TPU v7x, 32 devices: a whole 2x2x4 slice. The times are simulated.
32 devices in a mesh: groups: 1, section: 2 (over x), axial: 16 (over z, y, core).
Axes of the slice: x: 2, y: 2, z: 4, core: 2. Of those that a mesh axis runs over, the one named last changes fastest.
Arguments:
- pair_in: bfloat16 [4, 128, 128, 128], P('groups', 'axial'), may hold values from -6 to 6
- crop_mask: int32 [4, 128], P('groups'), may hold values 0 or 1
- proj_weights: bfloat16 [2, 5, 128, 128], P('section'), may hold values from -0.5 to 0.5
- out_weights: bfloat16 [2, 128, 128], P('section'), may hold values from -0.5 to 0.5
- up_weights: bfloat16 [2, 128, 512], P('section'), may hold values from -0.5 to 0.5
- down_weights: bfloat16 [2, 512, 128], P('section'), may hold values from -0.25 to 0.25
- norm_gains: bfloat16 [2, 3, 128], P('section'), may hold values from 0.099609375 to 1.8984375
Outputs:
- pair_out: bfloat16 [4, 128, 128, 128], P(('groups', 'section'), 'axial')
Inputs may be any that keep to these rules, and one draw needn't show every extreme that they name: `crop_mask`: 1 marks a residue inside the crop, 0 a padded one.
All inputs are finite; a program needn't handle non-finite values.
Results may differ from a plain program's by a relative error of at most 0.013.
Values may be sent and summed in bfloat16 or wider, within the bound.
A program may use at most 64 MiB of HBM per device.

v0:
```python
import functools

import jax
import jax.numpy as jnp
from jax import lax
from jax.experimental import pallas as pl
from jax.experimental.pallas import tpu as pltpu
from jax.sharding import PartitionSpec as P

epsilon = 1e-05


def normalize(values, axis_dim):
    center = values - jnp.mean(values, axis=axis_dim, keepdims=True)
    spread = jnp.mean(center * center, axis=axis_dim, keepdims=True)
    return center * lax.rsqrt(spread + epsilon)


def triangle(pieces):
    return jnp.einsum(
        "gcik,gcjk->gcij", pieces[0], pieces[1], preferred_element_type=jnp.float32
    ).astype(jnp.bfloat16)


def evo_block(current, mask_all, proj_mats, out_mat, up_mat, down_mat, gain_rows):
    row_count = current.shape[0]
    width = current.shape[1]
    channels = current.shape[2]
    group_count = lax.axis_size("axial")
    per_group = channels // group_count
    row_start = lax.axis_index("axial") * row_count
    mask_rows = lax.dynamic_slice_in_dim(mask_all, row_start, row_count)
    gain_vals = gain_rows.astype(jnp.float32)
    pair_f = current.astype(jnp.float32)
    normed = (normalize(pair_f, 2) * gain_vals[0]).astype(jnp.bfloat16)
    linear = jnp.einsum("rnd,edc->ecrn", normed, proj_mats[:4], preferred_element_type=jnp.float32)
    pair_mask = mask_rows[:, None] * mask_all[None, :]
    left_edge = (jax.nn.sigmoid(linear[1]) * linear[0] * pair_mask).astype(jnp.bfloat16)
    right_edge = (jax.nn.sigmoid(linear[3]) * linear[2] * pair_mask).astype(jnp.bfloat16)
    left_groups = left_edge.reshape(group_count, per_group, row_count, width)
    right_groups = right_edge.reshape(group_count, per_group, row_count, width)
    product = triangle(
        (
            lax.all_to_all(left_groups, "axial", split_axis=0, concat_axis=2, tiled=True),
            lax.all_to_all(right_groups, "axial", split_axis=0, concat_axis=2, tiled=True),
        )
    )
    restored = lax.all_to_all(product, "axial", split_axis=2, concat_axis=0, tiled=True).reshape(
        channels, row_count, width
    )
    tri_norm = (normalize(restored.astype(jnp.float32), 0) * gain_vals[1][:, None, None]).astype(
        jnp.bfloat16
    )
    update = jnp.einsum("crn,cd->rnd", tri_norm, out_mat, preferred_element_type=jnp.float32)
    gate_values = jax.nn.sigmoid(
        jnp.einsum("rnd,dc->rnc", normed, proj_mats[4], preferred_element_type=jnp.float32)
    )
    pair_mid = pair_f + gate_values * update
    trans_in = (normalize(pair_mid, 2) * gain_vals[2]).astype(jnp.bfloat16).reshape(-1, channels)
    hidden = jax.nn.relu(jnp.dot(trans_in, up_mat, preferred_element_type=jnp.float32)).astype(
        jnp.bfloat16
    )
    pair_new = pair_mid + jnp.dot(hidden, down_mat, preferred_element_type=jnp.float32).reshape(
        pair_mid.shape
    )
    return pair_new.astype(jnp.bfloat16)


MESH = pl.DeviceIdType.MESH


def sigmoid(values):
    return 0.5 * jnp.tanh(0.5 * values) + 0.5


def normalize_rows(values, gain):
    scale = 1.0 / values.shape[0]
    center = values - jnp.sum(values, axis=0, keepdims=True) * scale
    spread = jnp.sum(center * center, axis=0, keepdims=True) * scale
    return center * lax.rsqrt(spread + epsilon) * gain


def matmul(mat, values):
    return lax.dot_general(mat, values, (((1,), (0,)), ((), ())), preferred_element_type=jnp.float32)


def fused_kernel(
    sections,
    peers,
    halves,
    own_count,
    sub_rows,
    pair_ref,
    mask_ref,
    mask_smem,
    proj_ref,
    out_ref,
    up_ref,
    down_ref,
    gain_ref,
    result_ref,
    pair_buf,
    z_buf,
    normed_buf,
    gate_buf,
    edge_send,
    left_recv,
    right_recv,
    tri_send,
    tri_recv,
    left_f,
    right_f,
    tri_f,
    proj_all,
    out_all,
    up_all,
    down_all,
    gain_all,
    proj_t,
    out_t,
    up_t,
    down_t,
    gain_t,
    pair_sem,
    left_send_sem,
    left_recv_sem,
    right_send_sem,
    right_recv_sem,
    tri_send_sem,
    tri_recv_sem,
    weight_send_sem,
    weight_sem,
):
    section = lax.axis_index("section")
    me = lax.axis_index("axial")
    rows, width, channels = pair_buf.shape[1:]
    owners = peers // halves
    per_group = channels // owners
    my_half = me // owners
    my_owner = lax.rem(me, owners)
    steps = rows // sub_rows

    pair_copies = []
    for m in range(own_count):
        copy = pltpu.make_async_copy(
            pair_ref.at[section * own_count + m], pair_buf.at[m], pair_sem.at[m]
        )
        copy.start()
        pair_copies.append(copy)

    barrier = pltpu.get_barrier_semaphore()
    for k in range(1, peers):
        pl.semaphore_signal(
            barrier, inc=1, device_id={"axial": lax.rem(me + k, peers)}, device_id_type=MESH
        )
    for k in range(1, sections):
        pl.semaphore_signal(
            barrier,
            inc=1,
            device_id={"section": lax.rem(section + k, sections)},
            device_id_type=MESH,
        )
    weights = (
        (gain_ref, gain_all, None),
        (proj_ref, proj_all, (2, 2)),
        (proj_ref, proj_all, (0, 2)),
        (proj_ref, proj_all, (4, 1)),
        (out_ref, out_all, None),
        (up_ref, up_all, None),
        (down_ref, down_all, None),
    )

    def weight_part(ref, layer, span):
        return ref.at[layer] if span is None else ref.at[layer, pl.ds(*span)]

    for a, (source, gathered, span) in enumerate(weights):
        pltpu.make_async_copy(
            weight_part(source, 0, span),
            weight_part(gathered, section, span),
            weight_sem.at[a, section],
        ).start()

    def send_weights():
        copies = []
        for a, (_, gathered, span) in enumerate(weights):
            for k in range(1, sections):
                copy = pltpu.make_async_remote_copy(
                    src_ref=weight_part(gathered, section, span),
                    dst_ref=weight_part(gathered, section, span),
                    send_sem=weight_send_sem.at[a, k],
                    recv_sem=weight_sem.at[a, section],
                    device_id={"section": lax.rem(section + k, sections)},
                    device_id_type=MESH,
                )
                copy.start()
                copies.append(copy)
        return copies

    def wait_weight(a, layer):
        part = weight_part(weights[a][1], layer, weights[a][2])
        pltpu.make_async_copy(part, part, weight_sem.at[a, layer]).wait()

    def turned(values):
        return values.astype(jnp.float32).T.astype(jnp.bfloat16)

    def prepare_gains(layer):
        wait_weight(0, layer)
        for index in range(gain_t.shape[1]):
            row = gain_all[layer, index : index + 1, :].astype(jnp.float32)
            gain_t[layer, index] = jnp.broadcast_to(row, (width, channels)).T

    def prepare_proj(layer, side):
        wait_weight(2 - side, layer)
        for e in (2 * side, 2 * side + 1):
            proj_t[layer, e] = turned(proj_all[layer, e])

    def prepare_rest(layer):
        wait_weight(3, layer)
        proj_t[layer, 4] = turned(proj_all[layer, 4])
        for a in (4, 5, 6):
            wait_weight(a, layer)
        out_t[layer] = turned(out_all[layer])
        up_t[layer] = turned(up_all[layer])
        down_t[layer] = turned(down_all[layer])

    def prepare_all(layer):
        prepare_gains(layer)
        prepare_proj(layer, 1)
        prepare_proj(layer, 0)
        prepare_rest(layer)

    def wide_gain(layer, index):
        return jnp.concatenate([gain_t[layer, index]] * sub_rows, axis=1)

    def load_pair(m):
        pair_copies[m].wait()

        def step(q, carry):
            for s in range(sub_rows):
                r = q * sub_rows + s
                z_buf[m, q, :, s * width : (s + 1) * width] = pair_buf[m, r].astype(jnp.float32).T
            return carry

        lax.fori_loop(0, steps, step, 0, unroll=True)

    def phase_norm(layer, m):
        def step(q, carry):
            normed_buf[m, q] = normalize_rows(z_buf[m, q], wide_gain(layer, 0)).astype(jnp.bfloat16)
            return carry

        lax.fori_loop(0, steps, step, 0, unroll=True)

    def phase_edges(layer, m, side):
        row_mask = mask_ref[pl.ds(section * own_count + m, 1), :].astype(jnp.float32)

        def step(q, carry):
            values = normed_buf[m, q]
            masks = []
            for s in range(sub_rows):
                own = mask_smem[section * own_count + m, me * rows + q * sub_rows + s]
                masks.append(row_mask * own.astype(jnp.float32))
            pair_mask = jnp.concatenate(masks, axis=1)
            value = matmul(proj_t[layer, 2 * side], values)
            gate = matmul(proj_t[layer, 2 * side + 1], values)
            edge = sigmoid(gate) * value * pair_mask
            for s in range(sub_rows):
                part = edge[:, s * width : (s + 1) * width].reshape(owners, per_group, width)
                edge_send[m, :, side, q * sub_rows + s] = part.astype(jnp.bfloat16)
            return carry

        lax.fori_loop(0, steps, step, 0, unroll=True)

    def phase_gate(layer, m):
        def step(q, carry):
            gate_buf[m, q] = sigmoid(matmul(proj_t[layer, 4], normed_buf[m, q]))
            return carry

        lax.fori_loop(0, steps, step, 0, unroll=True)

    def left_copy(m, k):
        owner = lax.rem(my_owner + k, owners)
        return pltpu.make_async_remote_copy(
            src_ref=edge_send.at[m, owner, 0],
            dst_ref=left_recv.at[m, my_owner],
            send_sem=left_send_sem.at[m, k],
            recv_sem=left_recv_sem.at[m, my_owner],
            device_id={"axial": my_half * owners + owner},
            device_id_type=MESH,
        )

    def right_copy(slot, m, k):
        half = lax.rem(my_half + k // owners, halves)
        owner = lax.rem(my_owner + k % owners, owners)
        return pltpu.make_async_remote_copy(
            src_ref=edge_send.at[m, owner, 1],
            dst_ref=right_recv.at[slot, m, me],
            send_sem=right_send_sem.at[m, k],
            recv_sem=right_recv_sem.at[slot, m, me],
            device_id={"axial": half * owners + owner},
            device_id_type=MESH,
        )

    def tri_copy(m, k):
        owner = lax.rem(my_owner + k, owners)
        return pltpu.make_async_remote_copy(
            src_ref=tri_send.at[m, owner],
            dst_ref=tri_recv.at[m, my_owner],
            send_sem=tri_send_sem.at[m, k],
            recv_sem=tri_recv_sem.at[m, my_owner],
            device_id={"axial": my_half * owners + owner},
            device_id_type=MESH,
        )

    def send_right(slot, m):
        pltpu.make_async_copy(
            edge_send.at[m, my_owner, 1],
            right_recv.at[slot, m, me],
            right_recv_sem.at[slot, m, me],
        ).start()
        for k in range(peers - 1, 0, -1):
            right_copy(slot, m, k).start()

    def send_left(m):
        pltpu.make_async_copy(
            edge_send.at[m, my_owner, 0],
            left_recv.at[m, my_owner],
            left_recv_sem.at[m, my_owner],
        ).start()
        for k in range(owners - 1, 0, -1):
            left_copy(m, k).start()

    def wait_edges_sent(slot, m):
        for k in range(1, peers):
            right_copy(slot, m, k).wait_send()
        for k in range(1, owners):
            left_copy(m, k).wait_send()

    def send_tri(m):
        pltpu.make_async_copy(
            tri_send.at[m, my_owner], tri_recv.at[m, my_owner], tri_recv_sem.at[m, my_owner]
        ).start()
        for k in range(owners - 1, 0, -1):
            tri_copy(m, k).start()

    def wait_tri_sent(m):
        for k in range(1, owners):
            tri_copy(m, k).wait_send()

    def wait_left(m, g):
        pltpu.make_async_copy(left_recv.at[m, g], left_recv.at[m, g], left_recv_sem.at[m, g]).wait()

    def wait_right(slot, m, g):
        pltpu.make_async_copy(
            right_recv.at[slot, m, g], right_recv.at[slot, m, g], right_recv_sem.at[slot, m, g]
        ).wait()

    def wait_tri(m):
        for g in range(owners):
            pltpu.make_async_copy(tri_recv.at[m, g], tri_recv.at[m, g], tri_recv_sem.at[m, g]).wait()

    def phase_triangle(slot, m):
        for g in range(owners):
            wait_left(m, g)
            left_f[g * rows : (g + 1) * rows] = left_recv[m, g].astype(jnp.float32)
        for g in range(peers):
            wait_right(slot, m, g)
            right_f[g * rows : (g + 1) * rows] = right_recv[slot, m, g].astype(jnp.float32)
        for c in range(per_group):
            tri_f[:, c, :] = lax.dot_general(
                left_f[:, c, :].astype(jnp.bfloat16),
                right_f[:, c, :].astype(jnp.bfloat16),
                (((1,), (1,)), ((), ())),
                preferred_element_type=jnp.float32,
            )
        for g in range(owners):
            tri_send[m, g] = tri_f[g * rows : (g + 1) * rows].astype(jnp.bfloat16)

    def phase_update(layer, m, last):
        def step(q, carry):
            parts = []
            for s in range(sub_rows):
                part = tri_recv[m, :, q * sub_rows + s].astype(jnp.float32)
                parts.append(part.reshape(channels, width))
            tri = jnp.concatenate(parts, axis=1)
            tri_norm = normalize_rows(tri, wide_gain(layer, 1)).astype(jnp.bfloat16)
            mid = z_buf[m, q] + gate_buf[m, q] * matmul(out_t[layer], tri_norm)
            trans_in = normalize_rows(mid, wide_gain(layer, 2)).astype(jnp.bfloat16)
            hidden = jnp.maximum(matmul(up_t[layer], trans_in), 0.0).astype(jnp.bfloat16)
            fresh = mid + matmul(down_t[layer], hidden)
            if last:
                for s in range(sub_rows):
                    part = fresh[:, s * width : (s + 1) * width]
                    result_ref[m, q * sub_rows + s] = part.T.astype(jnp.bfloat16)
            else:
                z_buf[m, q] = fresh.astype(jnp.bfloat16).astype(jnp.float32)
            return carry

        lax.fori_loop(0, steps, step, 0, unroll=True)

    everyone = range(own_count)
    for m in everyone:
        load_pair(m)
    prepare_all(section)

    @pl.when(section == 0)
    def early_edges():
        for m in everyone:
            phase_norm(0, m)
            phase_edges(0, m, 1)
            phase_edges(0, m, 0)

    pl.semaphore_wait(barrier, peers - 1 + sections - 1)
    weight_copies = send_weights()

    @pl.when(section != 0)
    def late_norm():
        prepare_gains(0)
        for m in everyone:
            phase_norm(0, m)

    for m in everyone:
        for side in (1, 0):

            @pl.when(section != 0)
            def late_edges():
                if m == 0:
                    prepare_proj(0, side)
                phase_edges(0, m, side)

            if side:
                send_right(0, m)
            else:
                send_left(m)

    @pl.when(section != 0)
    def late_rest():
        prepare_rest(0)

    for m in everyone:
        phase_gate(0, m)

    for layer in range(1, sections):

        @pl.when(section != layer)
        def other_weights():
            prepare_all(layer)

    for layer in range(sections):
        last = layer == sections - 1
        for m in everyone:
            if layer > 0:
                wait_tri_sent(m)
            phase_triangle(layer % 2, m)
            send_tri(m)
        for m in everyone:
            wait_tri(m)
            phase_update(layer, m, last)
            wait_edges_sent(layer % 2, m)
            if not last:
                phase_norm(layer + 1, m)
                phase_edges(layer + 1, m, 1)
                send_right((layer + 1) % 2, m)
                phase_edges(layer + 1, m, 0)
                send_left(m)
        if not last:
            for m in everyone:
                phase_gate(layer + 1, m)
    for m in everyone:
        wait_tri_sent(m)
    for copy in weight_copies:
        copy.wait_send()


def fused_device(pair_in, crop_mask, proj_weights, out_weights, up_weights, down_weights, norm_gains):
    sections = lax.axis_size("section")
    peers = lax.axis_size("axial")
    micro_count, rows, width, channels = pair_in.shape
    own_count = micro_count // sections
    halves = half_count(pair_in)
    owners = peers // halves
    per_group = channels // owners
    sub_rows = 2 if rows % 2 == 0 else 1
    steps = rows // sub_rows
    lanes = sub_rows * width
    hidden = up_weights.shape[2]
    gains = norm_gains.shape[1]
    edge_kinds = proj_weights.shape[1]
    bf16, f32 = jnp.bfloat16, jnp.float32
    vmem = pl.BlockSpec(memory_space=pltpu.VMEM)
    hbm = pl.BlockSpec(memory_space=pltpu.HBM)
    dma = pltpu.SemaphoreType.DMA
    edge_shape = (own_count, owners, 2, rows, per_group, width)
    left_shape = (own_count, owners, rows, per_group, width)
    right_shape = (2, own_count, peers, rows, per_group, width)
    wide_shape = (own_count, steps, channels, lanes)
    return pl.pallas_call(
        functools.partial(fused_kernel, sections, peers, halves, own_count, sub_rows),
        out_shape=jax.ShapeDtypeStruct((own_count, rows, width, channels), bf16),
        in_specs=[hbm, vmem, pl.BlockSpec(memory_space=pltpu.SMEM)] + [hbm] * 5,
        out_specs=vmem,
        scratch_shapes=[
            pltpu.VMEM((own_count, rows, width, channels), bf16),
            pltpu.VMEM(wide_shape, f32),
            pltpu.VMEM(wide_shape, bf16),
            pltpu.VMEM(wide_shape, f32),
            pltpu.VMEM(edge_shape, bf16),
            pltpu.VMEM(left_shape, bf16),
            pltpu.VMEM(right_shape, bf16),
            pltpu.VMEM(left_shape, bf16),
            pltpu.VMEM(left_shape, bf16),
            pltpu.VMEM((owners * rows, per_group, width), f32),
            pltpu.VMEM((peers * rows, per_group, width), f32),
            pltpu.VMEM((owners * rows, per_group, width), f32),
            pltpu.VMEM((sections,) + proj_weights.shape[1:], bf16),
            pltpu.VMEM((sections,) + out_weights.shape[1:], bf16),
            pltpu.VMEM((sections,) + up_weights.shape[1:], bf16),
            pltpu.VMEM((sections,) + down_weights.shape[1:], bf16),
            pltpu.VMEM((sections,) + norm_gains.shape[1:], bf16),
            pltpu.VMEM((sections, edge_kinds, channels, channels), bf16),
            pltpu.VMEM((sections, channels, channels), bf16),
            pltpu.VMEM((sections, hidden, channels), bf16),
            pltpu.VMEM((sections, channels, hidden), bf16),
            pltpu.VMEM((sections, gains, channels, width), f32),
            dma((own_count,)),
            dma((own_count, owners)),
            dma((own_count, owners)),
            dma((own_count, peers)),
            dma((2, own_count, peers)),
            dma((own_count, owners)),
            dma((own_count, owners)),
            dma((7, sections)),
            dma((7, sections)),
        ],
        compiler_params=pltpu.CompilerParams(
            collective_id=0, has_side_effects=True, vmem_limit_bytes=67043328
        ),
    )(
        pair_in,
        crop_mask,
        crop_mask,
        proj_weights,
        out_weights,
        up_weights,
        down_weights,
        norm_gains,
    )


def half_count(pair_in):
    peers = lax.axis_size("axial")
    return 2 if peers % 2 == 0 and pair_in.shape[3] % (8 * (peers // 2)) == 0 else 1


def fits_fused(pair_in):
    rows, width, channels = pair_in.shape[1:]
    owners = lax.axis_size("axial") // half_count(pair_in)
    return channels % (8 * owners) == 0 and rows % 8 == 0 and width % 128 == 0


def per_device(pair_in, crop_mask, proj_weights, out_weights, up_weights, down_weights, norm_gains):
    if fits_fused(pair_in):
        return fused_device(
            pair_in, crop_mask, proj_weights, out_weights, up_weights, down_weights, norm_gains
        )
    section_index = lax.axis_index("section")
    section_count = lax.axis_size("section")
    micro_count = pair_in.shape[0]
    own_count = micro_count // section_count
    gathered = (
        lax.all_gather(proj_weights, "section", axis=0, tiled=True),
        lax.all_gather(out_weights, "section", axis=0, tiled=True),
        lax.all_gather(up_weights, "section", axis=0, tiled=True),
        lax.all_gather(down_weights, "section", axis=0, tiled=True),
        lax.all_gather(norm_gains, "section", axis=0, tiled=True),
    )
    own_pairs = lax.dynamic_slice_in_dim(pair_in, section_index * own_count, own_count, 0)
    own_masks = lax.dynamic_slice_in_dim(crop_mask, section_index * own_count, own_count, 0).astype(
        jnp.float32
    )
    outputs = []
    for member in range(own_count):
        current = own_pairs[member]
        for layer_index in range(section_count):
            current = evo_block(
                current,
                own_masks[member],
                gathered[0][layer_index],
                gathered[1][layer_index],
                gathered[2][layer_index],
                gathered[3][layer_index],
                gathered[4][layer_index],
            )
        outputs.append(current)
    return jnp.stack(outputs)


def solution(mesh):
    return jax.shard_map(
        per_device,
        mesh=mesh,
        in_specs=(
            P("groups", "axial", None, None),
            P("groups", None),
            P("section", None, None, None),
            P("section", None, None),
            P("section", None, None),
            P("section", None, None),
            P("section", None, None),
        ),
        out_specs=P(("groups", "section"), "axial", None, None),
        check_vma=False,
    )
```

profile of v0, /device:TPU:2, one launch (start us, length us, event | category | flops | bytes accessed | tf_op | source)
XLA Modules:
  0.0 76.4 jit_solution(15380271723972875382)
XLA Ops:
  0.0 74.5 %shard_map.73 = bf16[2,8,128,128]{3,2,1,0:T(8,128)(2,1)} custom-call(bf16[4,8,128,128]{3,2,1,0:T(8,128)(2,1)} %pair_ref.1, s32[4,128]{1,0:T(4,128)} %mask_smem.1, s32[4,128]{1,0:T(4,128)} %mask_smem.1, bf16[1,5,128,128]{3,2,1,0:T(8,128)(2,1)} %proj_ref.1, bf16[1,128,128]{2,1,0:T(8,128)(2,1)} %out_ref.1, bf16[1,128,512]{2,1,0:T(8,128)(2,1)} %up_ref.1, ...), custom_call_target="tpu_custom_call" | custom-call | tf_op jit(solution)/shard_map/pallas_call | solution.py:496
  74.5 1.9 %copy.9 = bf16[2,8,128,128]{3,2,1,0:T(8,128)(2,1)} copy(bf16[2,8,128,128]{3,2,1,0:T(8,128)(2,1)} %shard_map.73) | data formatting | bytes 1048576
where the time goes:
time: 76.6 us; the launch traced here: 76.4 us
  Pallas kernels  74.5 us (97%)
  local copies, waits for them, and re-layouts  1.89 us (2%)
    pallas_call x1, Pallas kernels, fused_device(): pl.pallas_call(functools.partial(fused_kernel, sections, peers, halves, o...  74.5 us
    unnamed x1, local copies, waits for them, and re-layouts  1.89 us

commit v1 on v0

v1 whole, which is shorter than its diff:
```python
import functools

import jax
import jax.numpy as jnp
from jax import lax
from jax.experimental import pallas as pl
from jax.experimental.pallas import tpu as pltpu
from jax.sharding import PartitionSpec as P

epsilon = 1e-05


def normalize(values, axis_dim):
    center = values - jnp.mean(values, axis=axis_dim, keepdims=True)
    spread = jnp.mean(center * center, axis=axis_dim, keepdims=True)
    return center * lax.rsqrt(spread + epsilon)


def triangle(pieces):
    return jnp.einsum(
        "gcik,gcjk->gcij", pieces[0], pieces[1], preferred_element_type=jnp.float32
    ).astype(jnp.bfloat16)


def evo_block(current, mask_all, proj_mats, out_mat, up_mat, down_mat, gain_rows):
    row_count = current.shape[0]
    width = current.shape[1]
    channels = current.shape[2]
    group_count = lax.axis_size("axial")
    per_group = channels // group_count
    row_start = lax.axis_index("axial") * row_count
    mask_rows = lax.dynamic_slice_in_dim(mask_all, row_start, row_count)
    gain_vals = gain_rows.astype(jnp.float32)
    pair_f = current.astype(jnp.float32)
    normed = (normalize(pair_f, 2) * gain_vals[0]).astype(jnp.bfloat16)
    linear = jnp.einsum("rnd,edc->ecrn", normed, proj_mats[:4], preferred_element_type=jnp.float32)
    pair_mask = mask_rows[:, None] * mask_all[None, :]
    left_edge = (jax.nn.sigmoid(linear[1]) * linear[0] * pair_mask).astype(jnp.bfloat16)
    right_edge = (jax.nn.sigmoid(linear[3]) * linear[2] * pair_mask).astype(jnp.bfloat16)
    left_groups = left_edge.reshape(group_count, per_group, row_count, width)
    right_groups = right_edge.reshape(group_count, per_group, row_count, width)
    product = triangle(
        (
            lax.all_to_all(left_groups, "axial", split_axis=0, concat_axis=2, tiled=True),
            lax.all_to_all(right_groups, "axial", split_axis=0, concat_axis=2, tiled=True),
        )
    )
    restored = lax.all_to_all(product, "axial", split_axis=2, concat_axis=0, tiled=True).reshape(
        channels, row_count, width
    )
    tri_norm = (normalize(restored.astype(jnp.float32), 0) * gain_vals[1][:, None, None]).astype(
        jnp.bfloat16
    )
    update = jnp.einsum("crn,cd->rnd", tri_norm, out_mat, preferred_element_type=jnp.float32)
    gate_values = jax.nn.sigmoid(
        jnp.einsum("rnd,dc->rnc", normed, proj_mats[4], preferred_element_type=jnp.float32)
    )
    pair_mid = pair_f + gate_values * update
    trans_in = (normalize(pair_mid, 2) * gain_vals[2]).astype(jnp.bfloat16).reshape(-1, channels)
    hidden = jax.nn.relu(jnp.dot(trans_in, up_mat, preferred_element_type=jnp.float32)).astype(
        jnp.bfloat16
    )
    pair_new = pair_mid + jnp.dot(hidden, down_mat, preferred_element_type=jnp.float32).reshape(
        pair_mid.shape
    )
    return pair_new.astype(jnp.bfloat16)


MESH = pl.DeviceIdType.MESH


def sigmoid(values):
    return 0.5 * jnp.tanh(0.5 * values) + 0.5


def normalize_rows(values, gain):
    scale = 1.0 / values.shape[0]
    center = values - jnp.sum(values, axis=0, keepdims=True) * scale
    spread = jnp.sum(center * center, axis=0, keepdims=True) * scale
    return center * lax.rsqrt(spread + epsilon) * gain


def matmul(mat, values):
    return lax.dot_general(mat, values, (((1,), (0,)), ((), ())), preferred_element_type=jnp.float32)


def fused_kernel(
    sections,
    ranks,
    halves,
    own_count,
    sub_rows,
    pair_ref,
    mask_ref,
    mask_smem,
    proj_ref,
    out_ref,
    up_ref,
    down_ref,
    gain_ref,
    result_ref,
    pair_buf,
    z_buf,
    normed_buf,
    gate_buf,
    edge_send,
    edge_recv,
    tri_send,
    tri_recv,
    left_f,
    right_f,
    tri_f,
    result_buf,
    proj_raw,
    out_raw,
    up_raw,
    down_raw,
    gain_all,
    proj_t,
    out_t,
    up_t,
    down_t,
    gain_t,
    pair_send_sem,
    pair_sem,
    edge_send_sem,
    edge_recv_sem,
    tri_send_sem,
    tri_recv_sem,
    result_send_sem,
    result_recv_sem,
    raw_sem,
    weight_send_sem,
    weight_pass_sem,
    weight_sem,
):
    section = lax.axis_index("section")
    axial = lax.axis_index("axial")
    span = ranks // sections
    group = axial // span
    place = lax.rem(axial, span)
    core = lax.rem(axial, 2)
    rank = section * span + place
    piece_rows, width, channels = pair_buf.shape[2:]
    rows = piece_rows * sections
    owners = ranks // halves
    per_group = channels // owners
    my_half = rank // owners
    my_owner = lax.rem(rank, owners)
    steps = piece_rows // sub_rows
    everyone = range(own_count)
    pieces = range(sections)

    def member(index):
        return {"section": index // span, "axial": group * span + lax.rem(index, span)}

    def part_of(t):
        return lax.rem(group + t, sections)

    def first_row(t, section_at, place_at):
        return (part_of(t) * span + place_at) * rows + section_at * piece_rows

    own_rows = pl.ds(section * piece_rows, piece_rows)

    for m in everyone:
        pltpu.make_async_copy(
            pair_ref.at[group * own_count + m, own_rows], pair_buf.at[m, 0], pair_sem.at[m, 0]
        ).start()
    raw_copies = [
        pltpu.make_async_copy(source, target, raw_sem.at[index])
        for index, (source, target) in enumerate(
            (
                (gain_ref.at[0], gain_all.at[section]),
                (proj_ref.at[0, pl.ds(2, 2)], proj_raw.at[pl.ds(2, 2)]),
                (proj_ref.at[0, pl.ds(0, 2)], proj_raw.at[pl.ds(0, 2)]),
                (proj_ref.at[0, pl.ds(4, 1)], proj_raw.at[pl.ds(4, 1)]),
                (out_ref.at[0], out_raw),
                (up_ref.at[0], up_raw),
                (down_ref.at[0], down_raw),
            )
        )
    ]
    for copy in raw_copies:
        copy.start()

    barrier = pltpu.get_barrier_semaphore()
    for k in range(1, ranks):
        pl.semaphore_signal(
            barrier, inc=1, device_id=member(lax.rem(rank + k, ranks)), device_id_type=MESH
        )
    for k in range(1, sections):
        for j in range(sections):
            pl.semaphore_signal(
                barrier,
                inc=1,
                device_id={
                    "section": lax.rem(section + j, sections),
                    "axial": part_of(k) * span + place,
                },
                device_id_type=MESH,
            )

    items = (
        (0, lambda layer: gain_all.at[layer]),
        (0, lambda layer: proj_t.at[layer, 2]),
        (1, lambda layer: proj_t.at[layer, 3]),
        (0, lambda layer: proj_t.at[layer, 0]),
        (1, lambda layer: proj_t.at[layer, 1]),
        (0, lambda layer: proj_t.at[layer, 4]),
        (1, lambda layer: out_t.at[layer]),
        (0, lambda layer: up_t.at[layer]),
        (1, lambda layer: down_t.at[layer]),
    )

    def item_copy(a, k):
        view = items[a][1](section)
        return pltpu.make_async_remote_copy(
            src_ref=view,
            dst_ref=view,
            send_sem=weight_send_sem.at[a, k],
            recv_sem=weight_sem.at[a, section],
            device_id={"section": lax.rem(section + k, sections)},
            device_id_type=MESH,
        )

    def item_pass(a, layer):
        view = items[a][1](layer)
        return pltpu.make_async_remote_copy(
            src_ref=view,
            dst_ref=view,
            send_sem=weight_pass_sem.at[a, layer],
            recv_sem=weight_sem.at[a, layer],
            device_id={"axial": axial + 1 - 2 * core},
            device_id_type=MESH,
        )

    def send_items(chosen):
        for side in range(2):

            @pl.when(core == side)
            def start():
                for a in chosen:
                    if items[a][0] == side:
                        for k in range(1, sections):
                            item_copy(a, k).start()

    def take_items(chosen, layer):
        for a in chosen:
            view = items[a][1](layer)
            pltpu.make_async_copy(view, view, weight_sem.at[a, layer]).wait()

            @pl.when(core == items[a][0])
            def pass_on():
                item_pass(a, layer).start()

    def finish_items():
        for side in range(2):

            @pl.when(core == side)
            def finish():
                for a, (owner, _) in enumerate(items):
                    if owner == side:
                        for k in range(1, sections):
                            item_copy(a, k).wait_send()
                        for k in range(1, sections):
                            item_pass(a, lax.rem(section + k, sections)).wait_send()

    def turned(values):
        return values.astype(jnp.float32).T.astype(jnp.bfloat16)

    def prepare_gains(layer):
        for index in range(gain_t.shape[1]):
            row = gain_all[layer, index : index + 1, :].astype(jnp.float32)
            gain_t[layer, index] = jnp.broadcast_to(row, (width, channels)).T

    def prepare_edges():
        raw_copies[0].wait()
        for pair in (1, 0):
            raw_copies[2 - pair].wait()
            for e in (2 * pair, 2 * pair + 1):
                proj_t[section, e] = turned(proj_raw[e])

    def prepare_rest():
        raw_copies[3].wait()
        proj_t[section, 4] = turned(proj_raw[4])
        for copy in raw_copies[4:]:
            copy.wait()
        out_t[section] = turned(out_raw[...])
        up_t[section] = turned(up_raw[...])
        down_t[section] = turned(down_raw[...])

    def wide_gain(layer, index):
        return jnp.concatenate([gain_t[layer, index]] * sub_rows, axis=1)

    def pair_copy(m, k):
        target = part_of(k)
        return pltpu.make_async_remote_copy(
            src_ref=pair_ref.at[target * own_count + m, own_rows],
            dst_ref=pair_buf.at[m, sections - k],
            send_sem=pair_send_sem.at[m, k],
            recv_sem=pair_sem.at[m, sections - k],
            device_id={"axial": target * span + place},
            device_id_type=MESH,
        )

    def load_pair(m, t):
        pltpu.make_async_copy(pair_buf.at[m, t], pair_buf.at[m, t], pair_sem.at[m, t]).wait()
        for q in range(steps):
            for i in range(sub_rows):
                z_buf[m, t, q, :, i * width : (i + 1) * width] = (
                    pair_buf[m, t, q * sub_rows + i].astype(jnp.float32).T
                )

    def phase_norm(layer, m, t):
        for q in range(steps):
            normed_buf[m, t, q] = normalize_rows(z_buf[m, t, q], wide_gain(layer, 0)).astype(
                jnp.bfloat16
            )

    def phase_edges(layer, m, t):
        crop = group * own_count + m
        row_mask = mask_ref[pl.ds(crop, 1), :].astype(jnp.float32)
        start = first_row(t, section, place)
        for q in range(steps):
            values = normed_buf[m, t, q]
            masks = []
            for i in range(sub_rows):
                own = mask_smem[crop, start + q * sub_rows + i]
                masks.append(row_mask * own.astype(jnp.float32))
            pair_mask = jnp.concatenate(masks, axis=1)
            for side in (1, 0):
                value = matmul(proj_t[layer, 2 * side], values)
                gate = matmul(proj_t[layer, 2 * side + 1], values)
                edge = sigmoid(gate) * value * pair_mask
                for i in range(sub_rows):
                    part = edge[:, i * width : (i + 1) * width].reshape(owners, per_group, width)
                    edge_send[m, t, :, side, q * sub_rows + i] = part.astype(jnp.bfloat16)

    def phase_gate(layer, m, t):
        for q in range(steps):
            gate_buf[m, t, q] = sigmoid(matmul(proj_t[layer, 4], normed_buf[m, t, q]))

    def rank_at(half_step, index):
        if halves == 1:
            return index
        return lax.rem(my_half + half_step, halves) * owners + index

    def edge_view(ref, half_step):
        return ref if half_step == 0 else ref.at[1]

    def edge_copy(slot, m, t, k):
        half_step = k // owners
        owner = lax.rem(my_owner + k % owners, owners)
        return pltpu.make_async_remote_copy(
            src_ref=edge_view(edge_send.at[m, t, owner], half_step),
            dst_ref=edge_view(edge_recv.at[slot, m, t, rank], half_step),
            send_sem=edge_send_sem.at[m, t, k],
            recv_sem=edge_recv_sem.at[slot, m, t, rank],
            device_id=member(rank_at(half_step, owner)),
            device_id_type=MESH,
        )

    def send_edges(slot, m, t):
        for k in range(ranks - 1, 0, -1):
            edge_copy(slot, m, t, k).start()
        pltpu.make_async_copy(
            edge_send.at[m, t, my_owner],
            edge_recv.at[slot, m, t, rank],
            edge_recv_sem.at[slot, m, t, rank],
        ).start()

    def wait_edges_sent(slot, m, t):
        for k in range(1, ranks):
            edge_copy(slot, m, t, k).wait_send()

    def tri_copy(m, k):
        owner = lax.rem(my_owner + k, owners)
        return pltpu.make_async_remote_copy(
            src_ref=tri_send.at[m, owner],
            dst_ref=tri_recv.at[m, my_owner],
            send_sem=tri_send_sem.at[m, k],
            recv_sem=tri_recv_sem.at[m, my_owner],
            device_id=member(my_half * owners + owner),
            device_id_type=MESH,
        )

    def send_tri(m):
        for k in range(owners - 1, 0, -1):
            tri_copy(m, k).start()
        pltpu.make_async_copy(
            tri_send.at[m, my_owner], tri_recv.at[m, my_owner], tri_recv_sem.at[m, my_owner]
        ).start()

    def wait_tri_sent(m):
        for k in range(1, owners):
            tri_copy(m, k).wait_send()

    def wait_tri(m):
        for g in range(owners):
            pltpu.make_async_copy(tri_recv.at[m, g], tri_recv.at[m, g], tri_recv_sem.at[m, g]).wait()

    def phase_triangle(slot, m):
        for t in pieces:
            for half_step in range(halves):
                for index in range(owners):
                    g = rank_at(half_step, index)
                    whole = edge_view(edge_recv.at[slot, m, t, g], half_step)
                    pltpu.make_async_copy(whole, whole, edge_recv_sem.at[slot, m, t, g]).wait()
                    start = first_row(t, g // span, g % span if halves == 1 else lax.rem(g, span))
                    right_f[pl.ds(start, piece_rows)] = edge_recv[slot, m, t, g, 1].astype(
                        jnp.float32
                    )
                    if half_step == 0:
                        at = index * rows + t * piece_rows
                        left_f[at : at + piece_rows] = edge_recv[slot, m, t, g, 0].astype(
                            jnp.float32
                        )
        for c in range(per_group):
            tri_f[:, c, :] = lax.dot_general(
                left_f[:, c, :].astype(jnp.bfloat16),
                right_f[:, c, :].astype(jnp.bfloat16),
                (((1,), (1,)), ((), ())),
                preferred_element_type=jnp.float32,
            )
        for g in range(owners):
            tri_send[m, g] = tri_f[g * rows : (g + 1) * rows].astype(jnp.bfloat16)

    def phase_update(layer, m, t, last):
        for q in range(steps):
            parts = []
            for i in range(sub_rows):
                part = tri_recv[m, :, t * piece_rows + q * sub_rows + i].astype(jnp.float32)
                parts.append(part.reshape(channels, width))
            tri = jnp.concatenate(parts, axis=1)
            tri_norm = normalize_rows(tri, wide_gain(layer, 1)).astype(jnp.bfloat16)
            mid = z_buf[m, t, q] + gate_buf[m, t, q] * matmul(out_t[layer], tri_norm)
            trans_in = normalize_rows(mid, wide_gain(layer, 2)).astype(jnp.bfloat16)
            hidden = jnp.maximum(matmul(up_t[layer], trans_in), 0.0).astype(jnp.bfloat16)
            fresh = mid + matmul(down_t[layer], hidden)
            if last:
                for i in range(sub_rows):
                    part = fresh[:, i * width : (i + 1) * width]
                    result_buf[m, t, q * sub_rows + i] = part.T.astype(jnp.bfloat16)
            else:
                z_buf[m, t, q] = fresh.astype(jnp.bfloat16).astype(jnp.float32)

    def result_copy(m, t):
        return pltpu.make_async_remote_copy(
            src_ref=result_buf.at[m, t],
            dst_ref=result_ref.at[m, own_rows],
            send_sem=result_send_sem.at[m, t],
            recv_sem=result_recv_sem.at[m, section],
            device_id={"section": group, "axial": part_of(t) * span + place},
            device_id_type=MESH,
        )

    def send_result(m, t):
        if t > 0:
            result_copy(m, t).start()
            return

        @pl.when(section == group)
        def keep():
            pltpu.make_async_copy(
                result_buf.at[m, t], result_ref.at[m, own_rows], result_recv_sem.at[m, section]
            ).start()

        @pl.when(section != group)
        def give():
            result_copy(m, t).start()

    def finish_results():
        for m in everyone:
            for t in pieces:
                if t > 0:
                    result_copy(m, t).wait_send()
                else:

                    @pl.when(section != group)
                    def given():
                        result_copy(m, t).wait_send()

            for s in range(sections):
                part = result_ref.at[m, pl.ds(s * piece_rows, piece_rows)]
                pltpu.make_async_copy(part, part, result_recv_sem.at[m, s]).wait()

    edge_items = range(5)
    rest_items = range(5, len(items))
    prepare_edges()
    pl.semaphore_wait(barrier, ranks - 1 + (sections - 1) * sections)
    send_items(edge_items)
    for m in everyone:
        for k in range(1, sections):
            pair_copy(m, k).start()
    prepare_gains(section)
    for m in everyone:
        load_pair(m, 0)
    prepare_rest()
    send_items(rest_items)

    @pl.when(section != 0)
    def first_weights():
        take_items(edge_items, 0)
        prepare_gains(0)

    for t in pieces:
        for m in everyone:
            if t > 0:
                load_pair(m, t)
            phase_norm(0, m, t)
            phase_edges(0, m, t)
            send_edges(0, m, t)

    @pl.when(section != 0)
    def other_weights():
        take_items(rest_items, 0)

    for layer in range(1, sections):

        @pl.when(section != layer)
        def later_weights():
            take_items(range(len(items)), layer)
            prepare_gains(layer)

    for m in everyone:
        for t in pieces:
            phase_gate(0, m, t)

    for layer in range(sections):
        last = layer == sections - 1
        for m in everyone:
            if layer > 0:
                wait_tri_sent(m)
            phase_triangle(layer % 2, m)
            send_tri(m)
        for m in everyone:
            wait_tri(m)
            for t in pieces:
                phase_update(layer, m, t, last)
                wait_edges_sent(layer % 2, m, t)
                if last:
                    send_result(m, t)
                else:
                    phase_norm(layer + 1, m, t)
                    phase_edges(layer + 1, m, t)
                    send_edges((layer + 1) % 2, m, t)
        if not last:
            for m in everyone:
                for t in pieces:
                    phase_gate(layer + 1, m, t)
    for m in everyone:
        wait_tri_sent(m)
        for k in range(1, sections):
            pair_copy(m, k).wait_send()
    finish_items()
    finish_results()


def fused_device(pair_in, crop_mask, proj_weights, out_weights, up_weights, down_weights, norm_gains):
    sections = lax.axis_size("section")
    ranks = lax.axis_size("axial")
    micro_count, rows, width, channels = pair_in.shape
    own_count = micro_count // sections
    halves = half_count(pair_in)
    owners = ranks // halves
    per_group = channels // owners
    piece_rows = rows // sections
    sub_rows = 2 if piece_rows % 2 == 0 else 1
    steps = piece_rows // sub_rows
    lanes = sub_rows * width
    hidden = up_weights.shape[2]
    gains = norm_gains.shape[1]
    edge_kinds = proj_weights.shape[1]
    bf16, f32 = jnp.bfloat16, jnp.float32
    vmem = pl.BlockSpec(memory_space=pltpu.VMEM)
    hbm = pl.BlockSpec(memory_space=pltpu.HBM)
    dma = pltpu.SemaphoreType.DMA
    piece = (piece_rows, per_group, width)
    rows_shape = (own_count, sections, piece_rows, width, channels)
    wide_shape = (own_count, sections, steps, channels, lanes)
    tri_shape = (own_count, owners, rows, per_group, width)
    return pl.pallas_call(
        functools.partial(fused_kernel, sections, ranks, halves, own_count, sub_rows),
        out_shape=jax.ShapeDtypeStruct((own_count, rows, width, channels), bf16),
        in_specs=[hbm, vmem, pl.BlockSpec(memory_space=pltpu.SMEM)] + [hbm] * 5,
        out_specs=hbm,
        scratch_shapes=[
            pltpu.VMEM(rows_shape, bf16),
            pltpu.VMEM(wide_shape, f32),
            pltpu.VMEM(wide_shape, bf16),
            pltpu.VMEM(wide_shape, f32),
            pltpu.VMEM((own_count, sections, owners, 2) + piece, bf16),
            pltpu.VMEM((2, own_count, sections, ranks, 2) + piece, bf16),
            pltpu.VMEM(tri_shape, bf16),
            pltpu.VMEM(tri_shape, bf16),
            pltpu.VMEM((owners * rows, per_group, width), f32),
            pltpu.VMEM((ranks * rows, per_group, width), f32),
            pltpu.VMEM((owners * rows, per_group, width), f32),
            pltpu.VMEM(rows_shape, bf16),
            pltpu.VMEM(proj_weights.shape[1:], bf16),
            pltpu.VMEM(out_weights.shape[1:], bf16),
            pltpu.VMEM(up_weights.shape[1:], bf16),
            pltpu.VMEM(down_weights.shape[1:], bf16),
            pltpu.VMEM((sections,) + norm_gains.shape[1:], bf16),
            pltpu.VMEM((sections, edge_kinds, channels, channels), bf16),
            pltpu.VMEM((sections, channels, channels), bf16),
            pltpu.VMEM((sections, hidden, channels), bf16),
            pltpu.VMEM((sections, channels, hidden), bf16),
            pltpu.VMEM((sections, gains, channels, width), f32),
            dma((own_count, sections)),
            dma((own_count, sections)),
            dma((own_count, sections, ranks)),
            dma((2, own_count, sections, ranks)),
            dma((own_count, owners)),
            dma((own_count, owners)),
            dma((own_count, sections)),
            dma((own_count, sections)),
            dma((7,)),
            dma((9, sections)),
            dma((9, sections)),
            dma((9, sections)),
        ],
        compiler_params=pltpu.CompilerParams(
            collective_id=0, has_side_effects=True, vmem_limit_bytes=67043328
        ),
    )(
        pair_in,
        crop_mask,
        crop_mask,
        proj_weights,
        out_weights,
        up_weights,
        down_weights,
        norm_gains,
    )


def half_count(pair_in):
    ranks = lax.axis_size("axial")
    return 2 if ranks % 2 == 0 and pair_in.shape[3] % (8 * ranks) else 1


def fits_fused(pair_in):
    rows, width, channels = pair_in.shape[1:]
    sections = lax.axis_size("section")
    ranks = lax.axis_size("axial")
    owners = ranks // half_count(pair_in)
    return (
        channels % (8 * owners) == 0
        and rows % sections == 0
        and width % 128 == 0
        and ranks % (2 * sections) == 0
    )


def per_device(pair_in, crop_mask, proj_weights, out_weights, up_weights, down_weights, norm_gains):
    if fits_fused(pair_in):
        return fused_device(
            pair_in, crop_mask, proj_weights, out_weights, up_weights, down_weights, norm_gains
        )
    section_index = lax.axis_index("section")
    section_count = lax.axis_size("section")
    micro_count = pair_in.shape[0]
    own_count = micro_count // section_count
    gathered = (
        lax.all_gather(proj_weights, "section", axis=0, tiled=True),
        lax.all_gather(out_weights, "section", axis=0, tiled=True),
        lax.all_gather(up_weights, "section", axis=0, tiled=True),
        lax.all_gather(down_weights, "section", axis=0, tiled=True),
        lax.all_gather(norm_gains, "section", axis=0, tiled=True),
    )
    own_pairs = lax.dynamic_slice_in_dim(pair_in, section_index * own_count, own_count, 0)
    own_masks = lax.dynamic_slice_in_dim(crop_mask, section_index * own_count, own_count, 0).astype(
        jnp.float32
    )
    outputs = []
    for member in range(own_count):
        current = own_pairs[member]
        for layer_index in range(section_count):
            current = evo_block(
                current,
                own_masks[member],
                gathered[0][layer_index],
                gathered[1][layer_index],
                gathered[2][layer_index],
                gathered[3][layer_index],
                gathered[4][layer_index],
            )
        outputs.append(current)
    return jnp.stack(outputs)


def solution(mesh):
    return jax.shard_map(
        per_device,
        mesh=mesh,
        in_specs=(
            P("groups", "axial", None, None),
            P("groups", None),
            P("section", None, None, None),
            P("section", None, None),
            P("section", None, None),
            P("section", None, None),
            P("section", None, None),
        ),
        out_specs=P(("groups", "section"), "axial", None, None),
        check_vma=False,
    )
```

time: 76.6 us -> 73.7 us (0.962)
  Pallas kernels: 74.5 us -> 71.6 us
    pallas_call x1, Pallas kernels: 74.5 us -> 71.6 us  [fused_device(): pl.pallas_call(functools.partial(fused_kernel, sections, ranks, halves, o...]
where the time goes in v1:
time: 73.7 us; the launch traced here: 73.5 us
  Pallas kernels  71.6 us (97%)
  local copies, waits for them, and re-layouts  1.89 us (3%)
    pallas_call x1, Pallas kernels, fused_device(): pl.pallas_call(functools.partial(fused_kernel, sections, ranks, halves, o...  71.6 us
    unnamed x1, local copies, waits for them, and re-layouts  1.89 us

profile of v1, /device:TPU:2, one launch (start us, length us, event | category | flops | bytes accessed | tf_op | source)
XLA Modules:
  0.0 73.5 jit_solution(14149103251305571570)
XLA Ops:
  0.0 71.6 %shard_map.73 = bf16[2,8,128,128]{3,2,1,0:T(8,128)(2,1)} custom-call(bf16[4,8,128,128]{3,2,1,0:T(8,128)(2,1)} %pair_ref.1, s32[4,128]{1,0:T(4,128)} %mask_smem.1, s32[4,128]{1,0:T(4,128)} %mask_smem.1, bf16[1,5,128,128]{3,2,1,0:T(8,128)(2,1)} %proj_ref.1, bf16[1,128,128]{2,1,0:T(8,128)(2,1)} %out_ref.1, bf16[1,128,512]{2,1,0:T(8,128)(2,1)} %up_ref.1, ...), custom_call_target="tpu_custom_call" | custom-call | tf_op jit(solution)/shard_map/pallas_call | solution.py:582
  71.6 1.9 %copy.9 = bf16[2,8,128,128]{3,2,1,0:T(8,128)(2,1)} copy(bf16[2,8,128,128]{3,2,1,0:T(8,128)(2,1)} %shard_map.73) | data formatting | bytes 1048576

commit v2 on v1

--- a/solution.py
+++ b/solution.py
@@ -244,14 +244,28 @@
                         for k in range(1, sections):
                             item_copy(a, k).start()
 
-    def take_items(chosen, layer):
-        for a in chosen:
-            view = items[a][1](layer)
-            pltpu.make_async_copy(view, view, weight_sem.at[a, layer]).wait()
-
-            @pl.when(core == items[a][0])
-            def pass_on():
-                item_pass(a, layer).start()
+    def wait_item(a, layer):
+        view = items[a][1](layer)
+        pltpu.make_async_copy(view, view, weight_sem.at[a, layer]).wait()
+
+    def pass_items(chosen, layer):
+        for side in range(2):
+
+            @pl.when(core == side)
+            def give_on():
+                for a in chosen:
+                    if items[a][0] == side:
+                        wait_item(a, layer)
+                        item_pass(a, layer).start()
+
+    def wait_items(chosen, layer):
+        for side in range(2):
+
+            @pl.when(core == side)
+            def receive():
+                for a in chosen:
+                    if items[a][0] != side:
+                        wait_item(a, layer)
 
     def finish_items():
         for side in range(2):
@@ -354,8 +368,8 @@
         return pltpu.make_async_remote_copy(
             src_ref=edge_view(edge_send.at[m, t, owner], half_step),
             dst_ref=edge_view(edge_recv.at[slot, m, t, rank], half_step),
-            send_sem=edge_send_sem.at[m, t, k],
-            recv_sem=edge_recv_sem.at[slot, m, t, rank],
+            send_sem=edge_send_sem.at[m, t],
+            recv_sem=edge_recv_sem.at[slot, m, t],
             device_id=member(rank_at(half_step, owner)),
             device_id_type=MESH,
         )
@@ -366,20 +380,26 @@
         pltpu.make_async_copy(
             edge_send.at[m, t, my_owner],
             edge_recv.at[slot, m, t, rank],
-            edge_recv_sem.at[slot, m, t, rank],
+            edge_recv_sem.at[slot, m, t],
         ).start()
 
-    def wait_edges_sent(slot, m, t):
-        for k in range(1, ranks):
-            edge_copy(slot, m, t, k).wait_send()
+    def wait_edges_sent(m, t):
+        left_over = (halves - 1) * owners
+        sent = edge_recv.at[0, m, t, pl.ds(0, owners - 1 + left_over // 2)]
+        pltpu.make_async_copy(sent, sent, edge_send_sem.at[m, t]).wait()
+
+    def wait_edges(slot, m, t):
+        left_over = (halves - 1) * owners
+        got = edge_recv.at[slot, m, t, pl.ds(0, owners + left_over // 2)]
+        pltpu.make_async_copy(got, got, edge_recv_sem.at[slot, m, t]).wait()
 
     def tri_copy(m, k):
         owner = lax.rem(my_owner + k, owners)
         return pltpu.make_async_remote_copy(
             src_ref=tri_send.at[m, owner],
             dst_ref=tri_recv.at[m, my_owner],
-            send_sem=tri_send_sem.at[m, k],
-            recv_sem=tri_recv_sem.at[m, my_owner],
+            send_sem=tri_send_sem.at[m],
+            recv_sem=tri_recv_sem.at[m],
             device_id=member(my_half * owners + owner),
             device_id_type=MESH,
         )
@@ -388,24 +408,22 @@
         for k in range(owners - 1, 0, -1):
             tri_copy(m, k).start()
         pltpu.make_async_copy(
-            tri_send.at[m, my_owner], tri_recv.at[m, my_owner], tri_recv_sem.at[m, my_owner]
+            tri_send.at[m, my_owner], tri_recv.at[m, my_owner], tri_recv_sem.at[m]
         ).start()
 
     def wait_tri_sent(m):
-        for k in range(1, owners):
-            tri_copy(m, k).wait_send()
+        sent = tri_recv.at[m, pl.ds(0, owners - 1)]
+        pltpu.make_async_copy(sent, sent, tri_send_sem.at[m]).wait()
 
     def wait_tri(m):
-        for g in range(owners):
-            pltpu.make_async_copy(tri_recv.at[m, g], tri_recv.at[m, g], tri_recv_sem.at[m, g]).wait()
+        pltpu.make_async_copy(tri_recv.at[m], tri_recv.at[m], tri_recv_sem.at[m]).wait()
 
     def phase_triangle(slot, m):
         for t in pieces:
+            wait_edges(slot, m, t)
             for half_step in range(halves):
                 for index in range(owners):
                     g = rank_at(half_step, index)
-                    whole = edge_view(edge_recv.at[slot, m, t, g], half_step)
-                    pltpu.make_async_copy(whole, whole, edge_recv_sem.at[slot, m, t, g]).wait()
                     start = first_row(t, g // span, g % span if halves == 1 else lax.rem(g, span))
                     right_f[pl.ds(start, piece_rows)] = edge_recv[slot, m, t, g, 1].astype(
                         jnp.float32
@@ -488,39 +506,68 @@
     rest_items = range(5, len(items))
     prepare_edges()
     pl.semaphore_wait(barrier, ranks - 1 + (sections - 1) * sections)
-    send_items(edge_items)
+
+    @pl.when(section == 0)
+    def first_items():
+        send_items(edge_items)
+
+    for k in range(1, sections):
+        pair_copy(0, k).start()
+    prepare_gains(section)
+
+    @pl.when(section != 0)
+    def other_items():
+        prepare_rest()
+        send_items(range(len(items)))
+
     for m in everyone:
+        load_pair(m, 0)
+
+    @pl.when(section != 0)
+    def first_weights():
+        pass_items(edge_items, 0)
+        wait_items(edge_items, 0)
+        prepare_gains(0)
+
+    phase_norm(0, 0, 0)
+    phase_edges(0, 0, 0)
+    send_edges(0, 0, 0)
+    for m in everyone[1:]:
         for k in range(1, sections):
             pair_copy(m, k).start()
-    prepare_gains(section)
+
+    @pl.when(section == 0)
+    def second_items():
+        prepare_rest()
+        send_items(rest_items)
+
+    for m in everyone[1:]:
+        phase_norm(0, m, 0)
+        phase_edges(0, m, 0)
+    for other in range(1, sections):
+
+        @pl.when(section != other)
+        def relay_later():
+            pass_items(range(len(items)), other)
+
     for m in everyone:
-        load_pair(m, 0)
-    prepare_rest()
-    send_items(rest_items)
-
-    @pl.when(section != 0)
-    def first_weights():
-        take_items(edge_items, 0)
-        prepare_gains(0)
-
-    for t in pieces:
-        for m in everyone:
-            if t > 0:
-                load_pair(m, t)
+        for t in pieces[1:]:
+            load_pair(m, t)
             phase_norm(0, m, t)
             phase_edges(0, m, t)
             send_edges(0, m, t)
+        if m == 0:
+
+            @pl.when(section != 0)
+            def relay_first():
+                pass_items(rest_items, 0)
+
+        if m + 1 < own_count:
+            send_edges(0, m + 1, 0)
 
     @pl.when(section != 0)
     def other_weights():
-        take_items(rest_items, 0)
-
-    for layer in range(1, sections):
-
-        @pl.when(section != layer)
-        def later_weights():
-            take_items(range(len(items)), layer)
-            prepare_gains(layer)
+        wait_items(rest_items, 0)
 
     for m in everyone:
         for t in pieces:
@@ -533,11 +580,19 @@
                 wait_tri_sent(m)
             phase_triangle(layer % 2, m)
             send_tri(m)
+        if layer == 0:
+            for other in range(1, sections):
+
+                @pl.when(section != other)
+                def later_weights():
+                    wait_items(range(len(items)), other)
+                    prepare_gains(other)
+
         for m in everyone:
             wait_tri(m)
             for t in pieces:
                 phase_update(layer, m, t, last)
-                wait_edges_sent(layer % 2, m, t)
+                wait_edges_sent(m, t)
                 if last:
                     send_result(m, t)
                 else:
@@ -609,10 +664,10 @@
             pltpu.VMEM((sections, gains, channels, width), f32),
             dma((own_count, sections)),
             dma((own_count, sections)),
-            dma((own_count, sections, ranks)),
-            dma((2, own_count, sections, ranks)),
-            dma((own_count, owners)),
-            dma((own_count, owners)),
+            dma((own_count, sections)),
+            dma((2, own_count, sections)),
+            dma((own_count,)),
+            dma((own_count,)),
             dma((own_count, sections)),
             dma((own_count, sections)),
             dma((7,)),

time: 73.7 us -> 66.8 us (0.906)
  Pallas kernels: 71.6 us -> 64.7 us
    pallas_call x1, Pallas kernels: 71.6 us -> 64.7 us  [fused_device(): pl.pallas_call(functools.partial(fused_kernel, sections, ranks, halves, o...]
where the time goes in v2:
time: 66.8 us; the launch traced here: 66.6 us
  Pallas kernels  64.7 us (97%)
  local copies, waits for them, and re-layouts  1.89 us (3%)
    pallas_call x1, Pallas kernels, fused_device(): pl.pallas_call(functools.partial(fused_kernel, sections, ranks, halves, o...  64.7 us
    unnamed x1, local copies, waits for them, and re-layouts  1.89 us

profile of v2, /device:TPU:2, one launch (start us, length us, event | category | flops | bytes accessed | tf_op | source)
XLA Modules:
  0.0 66.6 jit_solution(9215871198552225021)
XLA Ops:
  0.0 64.7 %shard_map.73 = bf16[2,8,128,128]{3,2,1,0:T(8,128)(2,1)} custom-call(bf16[4,8,128,128]{3,2,1,0:T(8,128)(2,1)} %pair_ref.1, s32[4,128]{1,0:T(4,128)} %mask_smem.1, s32[4,128]{1,0:T(4,128)} %mask_smem.1, bf16[1,5,128,128]{3,2,1,0:T(8,128)(2,1)} %proj_ref.1, bf16[1,128,128]{2,1,0:T(8,128)(2,1)} %out_ref.1, bf16[1,128,512]{2,1,0:T(8,128)(2,1)} %up_ref.1, ...), custom_call_target="tpu_custom_call" | custom-call | tf_op jit(solution)/shard_map/pallas_call | solution.py:637
  64.7 1.9 %copy.9 = bf16[2,8,128,128]{3,2,1,0:T(8,128)(2,1)} copy(bf16[2,8,128,128]{3,2,1,0:T(8,128)(2,1)} %shard_map.73) | data formatting | bytes 1048576

commit v3 on v2

--- a/solution.py
+++ b/solution.py
@@ -201,15 +201,15 @@
             )
 
     items = (
-        (0, lambda layer: gain_all.at[layer]),
-        (0, lambda layer: proj_t.at[layer, 2]),
+        (1, lambda layer: gain_all.at[layer]),
+        (1, lambda layer: proj_t.at[layer, 2]),
         (1, lambda layer: proj_t.at[layer, 3]),
-        (0, lambda layer: proj_t.at[layer, 0]),
+        (1, lambda layer: proj_t.at[layer, 0]),
         (1, lambda layer: proj_t.at[layer, 1]),
-        (0, lambda layer: proj_t.at[layer, 4]),
+        (1, lambda layer: proj_t.at[layer, 4]),
         (1, lambda layer: out_t.at[layer]),
         (0, lambda layer: up_t.at[layer]),
-        (1, lambda layer: down_t.at[layer]),
+        (0, lambda layer: down_t.at[layer]),
     )
 
     def item_copy(a, k):
@@ -444,23 +444,31 @@
             tri_send[m, g] = tri_f[g * rows : (g + 1) * rows].astype(jnp.bfloat16)
 
     def phase_update(layer, m, t, last):
-        for q in range(steps):
+        span_q = range(steps)
+
+        def tri_at(q):
             parts = []
             for i in range(sub_rows):
                 part = tri_recv[m, :, t * piece_rows + q * sub_rows + i].astype(jnp.float32)
                 parts.append(part.reshape(channels, width))
-            tri = jnp.concatenate(parts, axis=1)
-            tri_norm = normalize_rows(tri, wide_gain(layer, 1)).astype(jnp.bfloat16)
-            mid = z_buf[m, t, q] + gate_buf[m, t, q] * matmul(out_t[layer], tri_norm)
-            trans_in = normalize_rows(mid, wide_gain(layer, 2)).astype(jnp.bfloat16)
-            hidden = jnp.maximum(matmul(up_t[layer], trans_in), 0.0).astype(jnp.bfloat16)
-            fresh = mid + matmul(down_t[layer], hidden)
+            return jnp.concatenate(parts, axis=1)
+
+        gain_tri, gain_in = wide_gain(layer, 1), wide_gain(layer, 2)
+        tri_norm = [normalize_rows(tri_at(q), gain_tri).astype(jnp.bfloat16) for q in span_q]
+        update = [matmul(out_t[layer], tri_norm[q]) for q in span_q]
+        mid = [z_buf[m, t, q] + gate_buf[m, t, q] * update[q] for q in span_q]
+        trans_in = [normalize_rows(mid[q], gain_in).astype(jnp.bfloat16) for q in span_q]
+        hidden = [
+            jnp.maximum(matmul(up_t[layer], trans_in[q]), 0.0).astype(jnp.bfloat16) for q in span_q
+        ]
+        fresh = [mid[q] + matmul(down_t[layer], hidden[q]) for q in span_q]
+        for q in span_q:
             if last:
                 for i in range(sub_rows):
-                    part = fresh[:, i * width : (i + 1) * width]
+                    part = fresh[q][:, i * width : (i + 1) * width]
                     result_buf[m, t, q * sub_rows + i] = part.T.astype(jnp.bfloat16)
             else:
-                z_buf[m, t, q] = fresh.astype(jnp.bfloat16).astype(jnp.float32)
+                z_buf[m, t, q] = fresh[q].astype(jnp.bfloat16).astype(jnp.float32)
 
     def result_copy(m, t):
         return pltpu.make_async_remote_copy(
@@ -636,9 +644,9 @@
     tri_shape = (own_count, owners, rows, per_group, width)
     return pl.pallas_call(
         functools.partial(fused_kernel, sections, ranks, halves, own_count, sub_rows),
-        out_shape=jax.ShapeDtypeStruct((own_count, rows, width, channels), bf16),
+        out_shape=pltpu.VMEM((own_count, rows, width, channels), bf16),
         in_specs=[hbm, vmem, pl.BlockSpec(memory_space=pltpu.SMEM)] + [hbm] * 5,
-        out_specs=hbm,
+        out_specs=vmem,
         scratch_shapes=[
             pltpu.VMEM(rows_shape, bf16),
             pltpu.VMEM(wide_shape, f32),
@@ -676,7 +684,7 @@
             dma((9, sections)),
         ],
         compiler_params=pltpu.CompilerParams(
-            collective_id=0, has_side_effects=True, vmem_limit_bytes=67043328
+            collective_id=0, has_side_effects=True, vmem_limit_bytes=67043328 - 2 * own_count * rows * width * channels
         ),
     )(
         pair_in,

time: 66.8 us -> 64.4 us (0.964)
  Pallas kernels: 64.7 us -> 63.4 us
  local copies, waits for them, and re-layouts: 1.89 us -> 0.8 us
    pallas_call x1, Pallas kernels: 64.7 us -> 63.4 us  [fused_device(): pl.pallas_call(functools.partial(fused_kernel, sections, ranks, halves, o...]
    unnamed x1, local copies, waits for them, and re-layouts: 1.89 us -> 0.8 us
where the time goes in v3:
time: 64.4 us; the launch traced here: 64.2 us
  Pallas kernels  63.4 us (98%)
  local copies, waits for them, and re-layouts  0.8 us (1%)
    pallas_call x1, Pallas kernels, fused_device(): pl.pallas_call(functools.partial(fused_kernel, sections, ranks, halves, o...  63.4 us

profile of v3, /device:TPU:2, one launch (start us, length us, event | category | flops | bytes accessed | tf_op | source)
XLA Modules:
  0.0 64.2 jit_solution(679534669461388531)
XLA Ops:
  0.0 63.4 %shard_map.73 = bf16[2,8,128,128]{3,2,1,0:T(8,128)(2,1)S(1)} custom-call(bf16[4,8,128,128]{3,2,1,0:T(8,128)(2,1)} %pair_ref.1, s32[4,128]{1,0:T(4,128)} %mask_smem.1, s32[4,128]{1,0:T(4,128)} %mask_smem.1, bf16[1,5,128,128]{3,2,1,0:T(8,128)(2,1)} %proj_ref.1, bf16[1,128,128]{2,1,0:T(8,128)(2,1)} %out_ref.1, bf16[1,128,512]{2,1,0:T(8,128)(2,1)} %up_ref.1, ...), custom_call_target="tpu_custom_call" | custom-call | tf_op jit(solution)/shard_map/pallas_call | solution.py:645
  63.4 0.8 %copy.9 = bf16[2,8,128,128]{3,2,1,0:T(8,128)(2,1)} copy(bf16[2,8,128,128]{3,2,1,0:T(8,128)(2,1)S(1)} %shard_map.73) | data formatting | bytes 1048576

commit v4 on v3

--- a/solution.py
+++ b/solution.py
@@ -393,55 +393,78 @@
         got = edge_recv.at[slot, m, t, pl.ds(0, owners + left_over // 2)]
         pltpu.make_async_copy(got, got, edge_recv_sem.at[slot, m, t]).wait()
 
-    def tri_copy(m, k):
+    def tri_copy(m, t, k):
         owner = lax.rem(my_owner + k, owners)
         return pltpu.make_async_remote_copy(
-            src_ref=tri_send.at[m, owner],
-            dst_ref=tri_recv.at[m, my_owner],
-            send_sem=tri_send_sem.at[m],
-            recv_sem=tri_recv_sem.at[m],
+            src_ref=tri_send.at[m, t, owner],
+            dst_ref=tri_recv.at[m, t, my_owner],
+            send_sem=tri_send_sem.at[m, t],
+            recv_sem=tri_recv_sem.at[m, t],
             device_id=member(my_half * owners + owner),
             device_id_type=MESH,
         )
 
-    def send_tri(m):
+    def send_tri(m, t):
         for k in range(owners - 1, 0, -1):
-            tri_copy(m, k).start()
+            tri_copy(m, t, k).start()
         pltpu.make_async_copy(
-            tri_send.at[m, my_owner], tri_recv.at[m, my_owner], tri_recv_sem.at[m]
+            tri_send.at[m, t, my_owner], tri_recv.at[m, t, my_owner], tri_recv_sem.at[m, t]
         ).start()
 
     def wait_tri_sent(m):
-        sent = tri_recv.at[m, pl.ds(0, owners - 1)]
-        pltpu.make_async_copy(sent, sent, tri_send_sem.at[m]).wait()
-
-    def wait_tri(m):
-        pltpu.make_async_copy(tri_recv.at[m], tri_recv.at[m], tri_recv_sem.at[m]).wait()
-
-    def phase_triangle(slot, m):
+        for t in pieces:
+            sent = tri_recv.at[m, t, pl.ds(0, owners - 1)]
+            pltpu.make_async_copy(sent, sent, tri_send_sem.at[m, t]).wait()
+
+    def wait_tri(m, t):
+        pltpu.make_async_copy(tri_recv.at[m, t], tri_recv.at[m, t], tri_recv_sem.at[m, t]).wait()
+
+    def phase_triangle(slot, m, order):
+        columns = [slice(w * 128, (w + 1) * 128) for w in range(width // 128)]
+        piece_lines = piece_rows * per_group
+
+        def spread(target, at, values):
+            for w, lanes in enumerate(columns):
+                target[w, pl.ds(at, piece_lines)] = (
+                    values[:, :, lanes].astype(jnp.float32).reshape(piece_lines, 128)
+                )
+
+        def channel(source, c, count):
+            lines = pl.ds(c, count, stride=per_group)
+            return jnp.concatenate(
+                [source[w, lines, :].astype(jnp.bfloat16) for w in range(len(columns))], axis=1
+            )
+
         for t in pieces:
             wait_edges(slot, m, t)
             for half_step in range(halves):
                 for index in range(owners):
                     g = rank_at(half_step, index)
                     start = first_row(t, g // span, g % span if halves == 1 else lax.rem(g, span))
-                    right_f[pl.ds(start, piece_rows)] = edge_recv[slot, m, t, g, 1].astype(
-                        jnp.float32
+                    spread(
+                        right_f,
+                        pl.multiple_of(start * per_group, 8),
+                        edge_recv[slot, m, t, g, 1],
                     )
                     if half_step == 0:
                         at = index * rows + t * piece_rows
-                        left_f[at : at + piece_rows] = edge_recv[slot, m, t, g, 0].astype(
-                            jnp.float32
-                        )
+                        spread(left_f, at * per_group, edge_recv[slot, m, t, g, 0])
         for c in range(per_group):
-            tri_f[:, c, :] = lax.dot_general(
-                left_f[:, c, :].astype(jnp.bfloat16),
-                right_f[:, c, :].astype(jnp.bfloat16),
+            product = lax.dot_general(
+                channel(left_f, c, owners * rows),
+                channel(right_f, c, ranks * rows),
                 (((1,), (1,)), ((), ())),
                 preferred_element_type=jnp.float32,
             )
-        for g in range(owners):
-            tri_send[m, g] = tri_f[g * rows : (g + 1) * rows].astype(jnp.bfloat16)
+            for w, lanes in enumerate(columns):
+                tri_f[w, pl.ds(c, owners * rows, stride=per_group), :] = product[:, lanes]
+        for t in order:
+            for g in range(owners):
+                at = (g * rows + t * piece_rows) * per_group
+                for w, lanes in enumerate(columns):
+                    part = tri_f[w, at : at + piece_lines].reshape(piece_rows, per_group, 128)
+                    tri_send[m, t, g, :, :, lanes] = part.astype(jnp.bfloat16)
+            send_tri(m, t)
 
     def phase_update(layer, m, t, last):
         span_q = range(steps)
@@ -449,7 +472,7 @@
         def tri_at(q):
             parts = []
             for i in range(sub_rows):
-                part = tri_recv[m, :, t * piece_rows + q * sub_rows + i].astype(jnp.float32)
+                part = tri_recv[m, t, :, q * sub_rows + i].astype(jnp.float32)
                 parts.append(part.reshape(channels, width))
             return jnp.concatenate(parts, axis=1)
 
@@ -583,11 +606,11 @@
 
     for layer in range(sections):
         last = layer == sections - 1
+        order = pieces[::-1] if last else pieces
         for m in everyone:
             if layer > 0:
                 wait_tri_sent(m)
-            phase_triangle(layer % 2, m)
-            send_tri(m)
+            phase_triangle(layer % 2, m, order)
         if layer == 0:
             for other in range(1, sections):
 
@@ -597,8 +620,8 @@
                     prepare_gains(other)
 
         for m in everyone:
-            wait_tri(m)
-            for t in pieces:
+            for t in order:
+                wait_tri(m, t)
                 phase_update(layer, m, t, last)
                 wait_edges_sent(m, t)
                 if last:
@@ -641,7 +664,7 @@
     piece = (piece_rows, per_group, width)
     rows_shape = (own_count, sections, piece_rows, width, channels)
     wide_shape = (own_count, sections, steps, channels, lanes)
-    tri_shape = (own_count, owners, rows, per_group, width)
+    tri_shape = (own_count, sections, owners) + piece
     return pl.pallas_call(
         functools.partial(fused_kernel, sections, ranks, halves, own_count, sub_rows),
         out_shape=pltpu.VMEM((own_count, rows, width, channels), bf16),
@@ -656,9 +679,9 @@
             pltpu.VMEM((2, own_count, sections, ranks, 2) + piece, bf16),
             pltpu.VMEM(tri_shape, bf16),
             pltpu.VMEM(tri_shape, bf16),
-            pltpu.VMEM((owners * rows, per_group, width), f32),
-            pltpu.VMEM((ranks * rows, per_group, width), f32),
-            pltpu.VMEM((owners * rows, per_group, width), f32),
+            pltpu.VMEM((width // 128, owners * rows * per_group, 128), f32),
+            pltpu.VMEM((width // 128, ranks * rows * per_group, 128), f32),
+            pltpu.VMEM((width // 128, owners * rows * per_group, 128), f32),
             pltpu.VMEM(rows_shape, bf16),
             pltpu.VMEM(proj_weights.shape[1:], bf16),
             pltpu.VMEM(out_weights.shape[1:], bf16),
@@ -674,8 +697,8 @@
             dma((own_count, sections)),
             dma((own_count, sections)),
             dma((2, own_count, sections)),
-            dma((own_count,)),
-            dma((own_count,)),
+            dma((own_count, sections)),
+            dma((own_count, sections)),
             dma((own_count, sections)),
             dma((own_count, sections)),
             dma((7,)),

time: 64.4 us -> 61.7 us (0.958)
  Pallas kernels: 63.4 us -> 60.7 us
    pallas_call x1, Pallas kernels: 63.4 us -> 60.7 us  [fused_device(): pl.pallas_call(functools.partial(fused_kernel, sections, ranks, halves, o...]
where the time goes in v4:
time: 61.7 us; the launch traced here: 61.5 us
  Pallas kernels  60.7 us (98%)
  local copies, waits for them, and re-layouts  0.8 us (1%)
    pallas_call x1, Pallas kernels, fused_device(): pl.pallas_call(functools.partial(fused_kernel, sections, ranks, halves, o...  60.7 us

profile of v4, /device:TPU:2, one launch (start us, length us, event | category | flops | bytes accessed | tf_op | source)
XLA Modules:
  0.0 61.5 jit_solution(1707867861450331271)
XLA Ops:
  0.0 60.7 %shard_map.73 = bf16[2,8,128,128]{3,2,1,0:T(8,128)(2,1)S(1)} custom-call(bf16[4,8,128,128]{3,2,1,0:T(8,128)(2,1)} %pair_ref.1, s32[4,128]{1,0:T(4,128)} %mask_smem.1, s32[4,128]{1,0:T(4,128)} %mask_smem.1, bf16[1,5,128,128]{3,2,1,0:T(8,128)(2,1)} %proj_ref.1, bf16[1,128,128]{2,1,0:T(8,128)(2,1)} %out_ref.1, bf16[1,128,512]{2,1,0:T(8,128)(2,1)} %up_ref.1, ...), custom_call_target="tpu_custom_call" | custom-call | tf_op jit(solution)/shard_map/pallas_call | solution.py:668
  60.7 0.8 %copy.9 = bf16[2,8,128,128]{3,2,1,0:T(8,128)(2,1)} copy(bf16[2,8,128,128]{3,2,1,0:T(8,128)(2,1)S(1)} %shard_map.73) | data formatting | bytes 1048576

commit v5 on v4

--- a/solution.py
+++ b/solution.py
@@ -100,6 +100,7 @@
     gain_ref,
     result_ref,
     pair_buf,
+    pair_stage,
     z_buf,
     normed_buf,
     gate_buf,
@@ -121,6 +122,7 @@
     up_t,
     down_t,
     gain_t,
+    pair_stage_sem,
     pair_send_sem,
     pair_sem,
     edge_send_sem,
@@ -162,10 +164,37 @@
 
     own_rows = pl.ds(section * piece_rows, piece_rows)
 
+    barrier = pltpu.get_barrier_semaphore()
+    for k in range(1, ranks):
+        pl.semaphore_signal(
+            barrier, inc=1, device_id=member(lax.rem(rank + k, ranks)), device_id_type=MESH
+        )
+    for k in range(1, sections):
+        for j in range(sections):
+            pl.semaphore_signal(
+                barrier,
+                inc=1,
+                device_id={
+                    "section": lax.rem(section + j, sections),
+                    "axial": part_of(k) * span + place,
+                },
+                device_id_type=MESH,
+            )
+
+    def stage_copy(m, k):
+        return pltpu.make_async_copy(
+            pair_ref.at[part_of(k) * own_count + m, own_rows],
+            pair_stage.at[m, k - 1],
+            pair_stage_sem.at[m, k - 1],
+        )
+
     for m in everyone:
         pltpu.make_async_copy(
             pair_ref.at[group * own_count + m, own_rows], pair_buf.at[m, 0], pair_sem.at[m, 0]
         ).start()
+    for m in everyone:
+        for k in range(1, sections):
+            stage_copy(m, k).start()
     raw_copies = [
         pltpu.make_async_copy(source, target, raw_sem.at[index])
         for index, (source, target) in enumerate(
@@ -183,23 +212,6 @@
     for copy in raw_copies:
         copy.start()
 
-    barrier = pltpu.get_barrier_semaphore()
-    for k in range(1, ranks):
-        pl.semaphore_signal(
-            barrier, inc=1, device_id=member(lax.rem(rank + k, ranks)), device_id_type=MESH
-        )
-    for k in range(1, sections):
-        for j in range(sections):
-            pl.semaphore_signal(
-                barrier,
-                inc=1,
-                device_id={
-                    "section": lax.rem(section + j, sections),
-                    "axial": part_of(k) * span + place,
-                },
-                device_id_type=MESH,
-            )
-
     items = (
         (1, lambda layer: gain_all.at[layer]),
         (1, lambda layer: proj_t.at[layer, 2]),
@@ -309,7 +321,7 @@
     def pair_copy(m, k):
         target = part_of(k)
         return pltpu.make_async_remote_copy(
-            src_ref=pair_ref.at[target * own_count + m, own_rows],
+            src_ref=pair_stage.at[m, k - 1],
             dst_ref=pair_buf.at[m, sections - k],
             send_sem=pair_send_sem.at[m, k],
             recv_sem=pair_sem.at[m, sections - k],
@@ -359,12 +371,22 @@
             return index
         return lax.rem(my_half + half_step, halves) * owners + index
 
+    def partner(k):
+        if owners & (owners - 1):
+            return lax.rem(my_owner + k, owners)
+        index, unit = 0, 1
+        while unit < owners:
+            bit = lax.rem(my_owner // unit, 2)
+            index += unit * (1 - bit if k // unit % 2 else bit)
+            unit *= 2
+        return index
+
     def edge_view(ref, half_step):
         return ref if half_step == 0 else ref.at[1]
 
     def edge_copy(slot, m, t, k):
         half_step = k // owners
-        owner = lax.rem(my_owner + k % owners, owners)
+        owner = partner(k % owners)
         return pltpu.make_async_remote_copy(
             src_ref=edge_view(edge_send.at[m, t, owner], half_step),
             dst_ref=edge_view(edge_recv.at[slot, m, t, rank], half_step),
@@ -394,7 +416,7 @@
         pltpu.make_async_copy(got, got, edge_recv_sem.at[slot, m, t]).wait()
 
     def tri_copy(m, t, k):
-        owner = lax.rem(my_owner + k, owners)
+        owner = partner(k)
         return pltpu.make_async_remote_copy(
             src_ref=tri_send.at[m, t, owner],
             dst_ref=tri_recv.at[m, t, my_owner],
@@ -543,6 +565,7 @@
         send_items(edge_items)
 
     for k in range(1, sections):
+        stage_copy(0, k).wait()
         pair_copy(0, k).start()
     prepare_gains(section)
 
@@ -565,6 +588,7 @@
     send_edges(0, 0, 0)
     for m in everyone[1:]:
         for k in range(1, sections):
+            stage_copy(m, k).wait()
             pair_copy(m, k).start()
 
     @pl.when(section == 0)
@@ -672,6 +696,7 @@
         out_specs=vmem,
         scratch_shapes=[
             pltpu.VMEM(rows_shape, bf16),
+            pltpu.VMEM((own_count, sections - 1) + rows_shape[2:], bf16),
             pltpu.VMEM(wide_shape, f32),
             pltpu.VMEM(wide_shape, bf16),
             pltpu.VMEM(wide_shape, f32),
@@ -693,6 +718,7 @@
             pltpu.VMEM((sections, hidden, channels), bf16),
             pltpu.VMEM((sections, channels, hidden), bf16),
             pltpu.VMEM((sections, gains, channels, width), f32),
+            dma((own_count, sections - 1)),
             dma((own_count, sections)),
             dma((own_count, sections)),
             dma((own_count, sections)),

time: 61.7 us -> 60.7 us (0.984)
  Pallas kernels: 60.7 us -> 59.7 us
    pallas_call x1, Pallas kernels: 60.7 us -> 59.7 us  [fused_device(): pl.pallas_call(functools.partial(fused_kernel, sections, ranks, halves, o...]
where the time goes in v5:
time: 60.7 us; the launch traced here: 60.5 us
  Pallas kernels  59.7 us (98%)
  local copies, waits for them, and re-layouts  0.8 us (1%)
    pallas_call x1, Pallas kernels, fused_device(): pl.pallas_call(functools.partial(fused_kernel, sections, ranks, halves, o...  59.7 us

profile of v5, /device:TPU:2, one launch (start us, length us, event | category | flops | bytes accessed | tf_op | source)
XLA Modules:
  0.0 60.5 jit_solution(1125839510003849692)
XLA Ops:
  0.0 59.7 %shard_map.73 = bf16[2,8,128,128]{3,2,1,0:T(8,128)(2,1)S(1)} custom-call(bf16[4,8,128,128]{3,2,1,0:T(8,128)(2,1)} %pair_ref.1, s32[4,128]{1,0:T(4,128)} %mask_smem.1, s32[4,128]{1,0:T(4,128)} %mask_smem.1, bf16[1,5,128,128]{3,2,1,0:T(8,128)(2,1)} %proj_ref.1, bf16[1,128,128]{2,1,0:T(8,128)(2,1)} %out_ref.1, bf16[1,128,512]{2,1,0:T(8,128)(2,1)} %up_ref.1, ...), custom_call_target="tpu_custom_call" | custom-call | tf_op jit(solution)/shard_map/pallas_call | solution.py:692
  59.7 0.8 %copy.9 = bf16[2,8,128,128]{3,2,1,0:T(8,128)(2,1)} copy(bf16[2,8,128,128]{3,2,1,0:T(8,128)(2,1)S(1)} %shard_map.73) | data formatting | bytes 1048576

commit v6 on v5

--- a/solution.py
+++ b/solution.py
@@ -224,13 +224,16 @@
         (0, lambda layer: down_t.at[layer]),
     )
 
+    def beyond(layer):
+        return lax.rem(layer - section + sections, sections) - 1 if sections > 2 else 0
+
     def item_copy(a, k):
         view = items[a][1](section)
         return pltpu.make_async_remote_copy(
             src_ref=view,
             dst_ref=view,
-            send_sem=weight_send_sem.at[a, k],
-            recv_sem=weight_sem.at[a, section],
+            send_sem=weight_send_sem.at[a, k - 1],
+            recv_sem=weight_sem.at[a, sections - 1 - k],
             device_id={"section": lax.rem(section + k, sections)},
             device_id_type=MESH,
         )
@@ -240,8 +243,8 @@
         return pltpu.make_async_remote_copy(
             src_ref=view,
             dst_ref=view,
-            send_sem=weight_pass_sem.at[a, layer],
-            recv_sem=weight_sem.at[a, layer],
+            send_sem=weight_pass_sem.at[a, beyond(layer)],
+            recv_sem=weight_sem.at[a, beyond(layer)],
             device_id={"axial": axial + 1 - 2 * core},
             device_id_type=MESH,
         )
@@ -258,7 +261,7 @@
 
     def wait_item(a, layer):
         view = items[a][1](layer)
-        pltpu.make_async_copy(view, view, weight_sem.at[a, layer]).wait()
+        pltpu.make_async_copy(view, view, weight_sem.at[a, beyond(layer)]).wait()
 
     def pass_items(chosen, layer):
         for side in range(2):
@@ -323,7 +326,7 @@
         return pltpu.make_async_remote_copy(
             src_ref=pair_stage.at[m, k - 1],
             dst_ref=pair_buf.at[m, sections - k],
-            send_sem=pair_send_sem.at[m, k],
+            send_sem=pair_send_sem.at[m, k - 1],
             recv_sem=pair_sem.at[m, sections - k],
             device_id={"axial": target * span + place},
             device_id_type=MESH,
@@ -719,7 +722,7 @@
             pltpu.VMEM((sections, channels, hidden), bf16),
             pltpu.VMEM((sections, gains, channels, width), f32),
             dma((own_count, sections - 1)),
-            dma((own_count, sections)),
+            dma((own_count, sections - 1)),
             dma((own_count, sections)),
             dma((own_count, sections)),
             dma((2, own_count, sections)),
@@ -728,9 +731,9 @@
             dma((own_count, sections)),
             dma((own_count, sections)),
             dma((7,)),
-            dma((9, sections)),
-            dma((9, sections)),
-            dma((9, sections)),
+            dma((9, sections - 1)),
+            dma((9, sections - 1)),
+            dma((9, sections - 1)),
         ],
         compiler_params=pltpu.CompilerParams(
             collective_id=0, has_side_effects=True, vmem_limit_bytes=67043328 - 2 * own_count * rows * width * channels

time: 60.7 us -> 60.4 us (level)
  no operation moved by 1% of the time
where the time goes in v6:
time: 60.4 us; the launch traced here: 60.2 us
  Pallas kernels  59.4 us (98%)
  local copies, waits for them, and re-layouts  0.8 us (1%)
    pallas_call x1, Pallas kernels, fused_device(): pl.pallas_call(functools.partial(fused_kernel, sections, ranks, halves, o...  59.4 us

profile of v6, /device:TPU:2, one launch (start us, length us, event | category | flops | bytes accessed | tf_op | source)
XLA Modules:
  0.0 60.2 jit_solution(11625166896504644161)
XLA Ops:
  0.0 59.4 %shard_map.73 = bf16[2,8,128,128]{3,2,1,0:T(8,128)(2,1)S(1)} custom-call(bf16[4,8,128,128]{3,2,1,0:T(8,128)(2,1)} %pair_ref.1, s32[4,128]{1,0:T(4,128)} %mask_smem.1, s32[4,128]{1,0:T(4,128)} %mask_smem.1, bf16[1,5,128,128]{3,2,1,0:T(8,128)(2,1)} %proj_ref.1, bf16[1,128,128]{2,1,0:T(8,128)(2,1)} %out_ref.1, bf16[1,128,512]{2,1,0:T(8,128)(2,1)} %up_ref.1, ...), custom_call_target="tpu_custom_call" | custom-call | tf_op jit(solution)/shard_map/pallas_call | solution.py:695
  59.5 0.8 %copy.9 = bf16[2,8,128,128]{3,2,1,0:T(8,128)(2,1)} copy(bf16[2,8,128,128]{3,2,1,0:T(8,128)(2,1)S(1)} %shard_map.73) | data formatting | bytes 1048576
